TPU v7x, 32 devices: a whole 2x2x4 slice. The times are simulated.
32 devices in a mesh: layer: 4 (over z), facet: 8 (over y, x, core).
Axes of the slice: x: 2, y: 2, z: 4, core: 2. Of those that a mesh axis runs over, the one named last changes fastest.
Arguments:
- model_strip: bfloat16 [8, 2, 64, 8192], P('facet', None, None, 'layer'), may hold values from -6 to 6
- screen_angle: bfloat16 [4, 8, 64, 8192], P('layer', 'facet'), may hold values from -3.140625 to 3.140625
- facet_window: float32 [8, 8192], P('facet'), may hold values from 0.04 to 0.16
- facet_shift: int32 [8], P('facet'), may hold values from 0 to 8191
- kernel_taps: float32 [7], replicated, may hold values from 0.2 to 0.6
- plane_angle: float32 [4, 8], P('layer'), may hold values from -3.140625 to 3.140625
- u_cell: int32 [4, 128, 512], P('layer', 'facet'), may hold values from 0 to 63
- v_cell: int32 [4, 128, 512], P('layer', 'facet'), may hold values from 0 to 63
- w_plane: int32 [4, 128, 512], P('layer', 'facet'), may hold values from 0 to 7
- observed: float32 [4, 128, 2, 512], P('layer', 'facet'), may hold values from -6 to 6
Outputs:
- residual: float32 [4, 128, 2, 512], P('layer', 'facet')
- gradient: float32 [8, 2, 64, 8192], P('facet', None, None, 'layer')
All inputs are finite; a program needn't handle non-finite values.
Results may differ from a plain program's by a relative error of at most 0.009.
Values may be sent and summed in bfloat16 or wider, within the bound.
A program may use at most 64 MiB of HBM per device.

v0:
```python
import math

import jax
import jax.numpy as jnp
from jax import lax
from jax.sharding import PartitionSpec as P

STRIP_LEN = 8192
SUB_ROWS = 64
STRIP_COLS = 64
PLANES = 8
SUBGRIDS = 128


back_gain = 8.0


def fourier_table(length):
    positions = jnp.arange(length, dtype=jnp.int32)
    turn_count = positions[:, None] * positions[None, :] % length
    angles = 2.0 * math.pi / length * turn_count.astype(jnp.float32)
    norm_scale = 1.0 / math.sqrt(length)
    return (jnp.stack([jnp.cos(angles), -jnp.sin(angles)]) * norm_scale).astype(jnp.bfloat16)


def twiddle():
    low_index = jnp.arange(SUB_ROWS, dtype=jnp.int32)
    high_index = jnp.arange(SUBGRIDS, dtype=jnp.int32)
    turn_count = low_index[:, None] * high_index[None, :] % STRIP_LEN
    angles = 2.0 * math.pi / STRIP_LEN * turn_count.astype(jnp.float32)
    return (jnp.cos(angles), -jnp.sin(angles))


def facet_factor(window, shift_cells):
    positions = jnp.arange(STRIP_LEN, dtype=jnp.int32)
    turn_count = positions * shift_cells % STRIP_LEN
    angles = 2.0 * math.pi / STRIP_LEN * turn_count.astype(jnp.float32)
    factor_real = (window * jnp.cos(angles)).reshape(SUBGRIDS, SUB_ROWS, 1)
    factor_imag = (-window * jnp.sin(angles)).reshape(SUBGRIDS, SUB_ROWS, 1)
    return (factor_real, factor_imag)


def forward(screened, window, shift_cells):
    grid_view = screened.reshape(2, STRIP_COLS, SUB_ROWS, SUBGRIDS)
    section_one = jnp.einsum(
        "tka,pcab->tpckb", fourier_table(SUB_ROWS), grid_view, preferred_element_type=jnp.float32
    )
    real_part = section_one[0, 0] - section_one[1, 1]
    imag_part = section_one[0, 1] + section_one[1, 0]
    twist_real, twist_imag = twiddle()
    mixed = jnp.stack(
        [
            real_part * twist_real - imag_part * twist_imag,
            real_part * twist_imag + imag_part * twist_real,
        ]
    ).astype(jnp.bfloat16)
    section_two = jnp.einsum(
        "tjb,pckb->tpjkc", fourier_table(SUBGRIDS), mixed, preferred_element_type=jnp.float32
    )
    spec_real = section_two[0, 0] - section_two[1, 1]
    spec_imag = section_two[0, 1] + section_two[1, 0]
    factor_real, factor_imag = facet_factor(window, shift_cells)
    return jnp.concatenate(
        [
            spec_real * factor_real - spec_imag * factor_imag,
            spec_real * factor_imag + spec_imag * factor_real,
        ],
        axis=2,
    ).astype(jnp.bfloat16)


def backward(all_grids, window, shift_cells, screen_phase):
    values = all_grids.astype(jnp.float32)
    grid_real = values[:, :, :STRIP_COLS]
    grid_imag = values[:, :, STRIP_COLS:]
    factor_real, factor_imag = facet_factor(window, shift_cells)
    spectral = jnp.stack(
        [
            grid_real * factor_real + grid_imag * factor_imag,
            grid_imag * factor_real - grid_real * factor_imag,
        ]
    ).astype(jnp.bfloat16)
    section_two = jnp.einsum(
        "tjb,pjkc->tpckb", fourier_table(SUBGRIDS), spectral, preferred_element_type=jnp.float32
    )
    half_real = section_two[0, 0] + section_two[1, 1]
    half_imag = section_two[0, 1] - section_two[1, 0]
    twist_real, twist_imag = twiddle()
    mixed = jnp.stack(
        [
            half_real * twist_real + half_imag * twist_imag,
            half_imag * twist_real - half_real * twist_imag,
        ]
    ).astype(jnp.bfloat16)
    section_one = jnp.einsum(
        "tka,pckb->tpcab", fourier_table(SUB_ROWS), mixed, preferred_element_type=jnp.float32
    )
    image_real = (section_one[0, 0] + section_one[1, 1]).reshape(STRIP_COLS, STRIP_LEN)
    image_imag = (section_one[0, 1] - section_one[1, 0]).reshape(STRIP_COLS, STRIP_LEN)
    phases = screen_phase.astype(jnp.float32)
    cosine = jnp.cos(phases)
    sine_part = jnp.sin(phases)
    return back_gain * jnp.stack(
        [image_real * cosine + image_imag * sine_part, image_imag * cosine - image_real * sine_part]
    )


def spread(cell_index, length, kernel_taps):
    tap_count = kernel_taps.shape[0]
    offset = (jnp.arange(length, dtype=jnp.int32)[None, :] - cell_index[:, None]) % length
    wanted = (jnp.arange(tap_count, dtype=jnp.int32) - tap_count // 2) % length
    matches = (offset[:, :, None] == wanted[None, None, :]).astype(jnp.float32)
    return jnp.sum(matches * kernel_taps, axis=2)


def adjoint_from(row_weights, column_weights, weighted):
    spread_cols = jnp.concatenate(
        [weighted[0][:, None] * column_weights, weighted[1][:, None] * column_weights], axis=1
    )
    return jnp.dot(row_weights.T, spread_cols, precision=lax.Precision.HIGHEST)


def degrid(subgrid, row_cells, column_cells, plane, observed_vis, angle_table, kernel_taps):
    row_weights = spread(row_cells, SUB_ROWS, kernel_taps)
    column_weights = spread(column_cells, STRIP_COLS, kernel_taps)
    kernel_rows = jnp.dot(row_weights, subgrid, precision=lax.Precision.HIGHEST)
    model_real = jnp.sum(kernel_rows[:, :STRIP_COLS] * column_weights, axis=1)
    model_imag = jnp.sum(kernel_rows[:, STRIP_COLS:] * column_weights, axis=1)
    plane_pick = (plane[:, None] == jnp.arange(PLANES, dtype=jnp.int32)[None, :]).astype(
        jnp.float32
    )
    phase_angle = jnp.sum(plane_pick * angle_table[None, :], axis=1)
    cosine = jnp.cos(phase_angle)
    sine_part = jnp.sin(phase_angle)
    residual_real = observed_vis[0] - (model_real * cosine - model_imag * sine_part)
    residual_imag = observed_vis[1] - (model_real * sine_part + model_imag * cosine)
    weighted = jnp.stack(
        [
            residual_real * cosine + residual_imag * sine_part,
            residual_imag * cosine - residual_real * sine_part,
        ]
    )
    return (jnp.stack([residual_real, residual_imag]), weighted, row_weights, column_weights)


def local(
    model_strip,
    screen_angle,
    facet_window,
    facet_shift,
    kernel_taps,
    plane_angle,
    u_cell,
    v_cell,
    w_plane,
    observed,
):
    strip_data = lax.all_gather(model_strip, "layer", axis=3, tiled=True)[0]
    phases = screen_angle[0, 0].astype(jnp.float32)
    cosine = jnp.cos(phases)
    sine_part = jnp.sin(phases)
    strip_values = strip_data.astype(jnp.float32)
    screened = jnp.stack(
        [
            strip_values[0] * cosine - strip_values[1] * sine_part,
            strip_values[0] * sine_part + strip_values[1] * cosine,
        ]
    ).astype(jnp.bfloat16)
    contrib = forward(screened, facet_window[0], facet_shift[0])
    received = lax.all_to_all(contrib, "facet", split_axis=0, concat_axis=0, tiled=True)
    owner_count = lax.axis_size("facet")
    per_owner = received.shape[0] // owner_count
    grids = jnp.sum(
        received.reshape(owner_count, per_owner, SUB_ROWS, 2 * STRIP_COLS).astype(jnp.float32),
        axis=0,
    )
    residual_vis, weighted, row_weights, column_weights = jax.vmap(
        degrid, in_axes=(0, 0, 0, 0, 0, None, None)
    )(grids, u_cell[0], v_cell[0], w_plane[0], observed[0], plane_angle[0], kernel_taps)
    adjoint = jax.vmap(adjoint_from)(row_weights, column_weights, weighted).astype(jnp.bfloat16)
    all_grids = lax.all_gather(adjoint, "facet", axis=0, tiled=True)
    term = backward(all_grids, facet_window[0], facet_shift[0], screen_angle[0, 0]).astype(
        jnp.bfloat16
    )
    pieces = lax.all_to_all(term[None], "layer", split_axis=3, concat_axis=0, tiled=True)
    gradient = jnp.sum(pieces.astype(jnp.float32), axis=0)[None]
    return (residual_vis[None], gradient)


def solution(mesh):
    return jax.shard_map(
        local,
        mesh=mesh,
        in_specs=(
            P("facet", None, None, "layer"),
            P("layer", "facet", None, None),
            P("facet", None),
            P("facet"),
            P(),
            P("layer", None),
            P("layer", "facet", None),
            P("layer", "facet", None),
            P("layer", "facet", None),
            P("layer", "facet", None, None),
        ),
        out_specs=(P("layer", "facet", None, None), P("facet", None, None, "layer")),
        check_vma=False,
    )
```

profile of v0, /device:TPU:0, one launch (start us, length us, event | category | flops | bytes accessed | tf_op | source)
XLA Modules:
  0.0 259.3 jit_solution(13630020163129976060)
XLA Ops:
  7.2 0.7 all-gather.3.cloned.1.call-update
  7.9 0.5 broadcast.531
  8.4 1.5 reduce.6
  10.7 1.5 copy.124
  12.5 0.3 sine_negate_fusion
  13.0 45.0 %all-gather.3.cloned.1.call-done = bf16[1,2,64,8192]{3,2,1,0:T(8,128)(2,1)} async-done(((bf16[1,2,64,2048]{3,2,1,0:T(8,128)(2,1)}), bf16[1,2,64,8192]{3,2,1,0:T(8,128)(2,1)}) %all-gather.3.cloned.1.call-update) | async-done | bytes 2097168 | tf_op jit(solution)/shard_map/all_gather | solution.py:158
  58.0 2.0 convert_element_type.143
  60.0 8.0 %fusion.51 = (bf16[8,8,64,128]{3,1,2,0:T(8,128)(2,1)S(1)}, bf16[8,8,64,128]{3,1,2,0:T(8,128)(2,1)S(1)}) fusion(f32[1,2,64,8192]{3,2,1,0:T(8,128)S(1)} %convert_element_type.143, bf16[1,1,64,8192]{3,2,1,0:T(8,128)(2,1)S(1)} %copy-done.2), kind=kLoop, calls=%fused_computation.93 | loop fusion | flops 4718592 | bytes 7340032
  68.0 0.3 copy.121
  68.2 0.3 copy.122
  68.5 1.2 convolution_bitcast_fusion.1
  69.7 1.1 subtract_convert_fusion.3
  70.9 1.2 convolution_bitcast_fusion.3
  72.1 1.1 subtract_convert_fusion.2
  73.2 0.2 pad_maximum_fusion
  73.4 3.4 %copy.96 = bf16[128,64,128]{2,1,0:T(8,128)(2,1)} copy(bf16[128,64,128]{0,1,2:T(8,128)(2,1)S(1)} %pad_maximum_fusion) | data formatting | bytes 4194304 | tf_op jit(solution)/shard_map/concatenate | solution.py:63
  76.8 4.5 %all-to-all-start = ((bf16[128,64,128]{2,1,0:T(8,128)(2,1)}), bf16[128,64,128]{2,1,0:T(8,128)(2,1)}, u32[]{:S(2)}, u32[]{:S(2)}) async-start(bf16[128,64,128]{2,1,0:T(8,128)(2,1)} %copy.96), calls=%async_computation | async-start | bytes 4194304 | tf_op jit(solution)/shard_map/all_to_all | solution.py:170
  81.3 0.2 all-gather.5.cloned.1.call-start
  81.6 1.6 add_select_fusion
  83.3 4.7 %select_reduce_fusion.1 = (f32[16,512,64]{1,2,0:T(8,128)}, f32[16,512,64]{1,2,0:T(8,128)S(1)}) fusion(f32[7]{0:T(128)S(1)} %copy-done.11, s32[16,512,64]{1,2,0:T(8,128)S(1)} %get-tuple-element.38, s32[7]{0:T(128)S(1)} %and_select_fusion, s32[16,512,64]{1,2,0:T(8,128)S(1)} %get-tuple-element.37), kind=kLoop, calls=%fused_computation.1 | loop fusion | flops 20971520 | bytes 8388664 | tf_op jit(solution)/shard_map/vmap()/reduce_sum | solution.py:113
  87.9 2.7 %copy.97 = f32[16,512,64]{2,1,0:T(8,128)} copy(f32[16,512,64]{1,2,0:T(8,128)S(1)} %get-tuple-element.11) | data formatting | bytes 4194304 | tf_op jit(solution)/shard_map/vmap()/reduce_sum | solution.py:113
  90.9 17.0 %all-to-all-done = bf16[128,64,128]{2,1,0:T(8,128)(2,1)} async-done(((bf16[128,64,128]{2,1,0:T(8,128)(2,1)}), bf16[128,64,128]{2,1,0:T(8,128)(2,1)}, u32[]{:S(2)}, u32[]{:S(2)}) %all-to-all-start) | async-done | bytes 2097184 | tf_op jit(solution)/shard_map/all_to_all | solution.py:170
  108.0 2.2 convert_reduce_fusion.1
  110.2 3.6 %fusion.108 = f32[16,512,128]{1,2,0:T(8,128)S(1)} fusion(f32[16,512,64]{1,2,0:T(8,128)S(1)} %copy-done, f32[16,64,128]{2,1,0:T(8,128)S(1)} %convert_reduce_fusion.1), kind=kOutput, calls=%fused_computation.183 | convolution fusion | flops 805306368 | bytes 6815744 | tf_op jit(solution)/shard_map/vmap()/dot_general | solution.py:126
  113.9 0.9 fusion.24
  114.9 1.2 copy-done.1
  116.1 2.5 broadcast_multiply_fusion.1
  118.6 4.1 %fusion.45 = bf16[16,64,128]{2,1,0:T(8,128)(2,1)} fusion(f32[16,512,64]{1,2,0:T(8,128)S(1)} %copy-done, f32[16,512,64]{2,1,0:T(8,128)S(1)} %get-tuple-element.30, f32[16,512,64]{2,1,0:T(8,128)S(1)} %get-tuple-element.29), kind=kOutput, calls=%fused_computation.89 | convolution fusion | flops 806486016 | bytes 6553600 | tf_op jit(solution)/shard_map/vmap()/dot_general | solution.py:120
  122.6 25.1 %all-gather.5.cloned.1.call-done = bf16[128,64,128]{2,1,0:T(8,128)(2,1)} async-done(((bf16[16,64,128]{2,1,0:T(8,128)(2,1)}), bf16[128,64,128]{2,1,0:T(8,128)(2,1)}) %all-gather.5.cloned.1.call-update) | async-done | bytes 2097168 | tf_op jit(solution)/shard_map/all_gather | solution.py:181
  147.8 4.1 %copy.99 = bf16[128,64,128]{0,1,2:T(8,128)(2,1)S(1)} copy(bf16[128,64,128]{2,1,0:T(8,128)(2,1)} %all-gather.5.cloned.1.call-done) | data formatting | bytes 4194304 | tf_op jit(solution)/shard_map/all_gather | solution.py:181
  151.9 0.4 convert_element_type.154
  152.3 0.6 fusion.48
  152.9 1.2 convolution_bitcast_fusion.2
  154.2 1.1 add_convert_fusion
  155.3 1.3 convolution_bitcast_fusion
  156.6 2.9 %slice_subtract_fusion = (f32[1,1,64,64,128]{4,3,0,2,1:T(8,128)}, f32[1,1,64,64,128]{4,3,0,2,1:T(8,128)}) fusion(f32[2,2,64,64,128]{4,3,0,2,1:T(8,128)S(1)} %convolution_bitcast_fusion), kind=kLoop, calls=%fused_computation.38 | loop fusion | flops 1048576 | bytes 12582912 | tf_op jit(solution)/shard_map/sub | solution.py:99
  159.5 1.7 add.275
  161.2 2.8 %sub.229 = f32[1,1,64,8192]{3,2,1,0:T(8,128)} reshape(f32[1,1,64,64,128]{4,3,0,2,1:T(8,128)} %get-tuple-element.21) | data formatting | bytes 4194304 | tf_op jit(solution)/shard_map/sub | solution.py:99
  164.0 8.8 %fusion.17 = (f32[1,1,64,8192]{3,2,1,0:T(8,128)S(1)}, f32[1,1,64,8192]{3,2,1,0:T(8,128)S(1)}) fusion(f32[1,1,64,8192]{3,2,1,0:T(8,128)} %sub.229, bf16[1,1,64,8192]{3,2,1,0:T(8,128)(2,1)S(1)} %copy-done.2, f32[1,1,64,8192]{3,2,1,0:T(8,128)S(1)} %add.275), kind=kLoop, calls=%fused_computation.34 | loop fusion | flops 3670016 | bytes 9437184 | tf_op jit(solution)/shard_map/add | solution.py:104
  172.8 0.3 fusion.4
  173.0 6.8 %copy.103 = bf16[1,2,64,8192]{2,1,0,3:T(2,128)(2,1)} copy(bf16[1,2,64,8192]{3,2,1,0:T(8,128)(2,1)S(1)} %fusion.4) | data formatting | bytes 4194304 | tf_op jit(solution)/shard_map/convert_element_type | solution.py:182
  179.9 5.9 %reshape.702 = bf16[4,2,131072]{2,1,0:T(2,128)(2,1)} reshape(bf16[8192,1,2,64]{3,2,1,0:T(2,128)(2,1)} %bitcast.221) | data formatting | bytes 4194304
  185.8 4.7 %all-to-all-start.1 = ((bf16[4,2,131072]{2,1,0:T(2,128)(2,1)}), bf16[4,2,131072]{2,1,0:T(2,128)(2,1)S(1)}, u32[]{:S(2)}, u32[]{:S(2)}) async-start(bf16[4,2,131072]{2,1,0:T(2,128)(2,1)} %reshape.702), calls=%async_computation.1 | async-start | bytes 4194304 | tf_op jit(solution)/shard_map/all_to_all | solution.py:185
  190.5 0.7 copy.104
  191.2 47.9 %all-to-all-done.1 = bf16[4,2,131072]{2,1,0:T(2,128)(2,1)S(1)} async-done(((bf16[4,2,131072]{2,1,0:T(2,128)(2,1)}), bf16[4,2,131072]{2,1,0:T(2,128)(2,1)S(1)}, u32[]{:S(2)}, u32[]{:S(2)}) %all-to-all-start.1) | async-done | bytes 2097184 | tf_op jit(solution)/shard_map/all_to_all | solution.py:185
  239.1 4.0 %reshape.703 = bf16[8192,1,2,64]{3,2,1,0:T(2,128)(2,1)} reshape(bf16[4,2,131072]{2,1,0:T(2,128)(2,1)S(1)} %all-to-all-done.1) | data formatting | bytes 4194304
  243.1 7.3 %convert_reduce_fusion = f32[2,64,2048]{1,0,2:T(2,128)S(1)} fusion(bf16[2,64,4,2048]{1,0,3,2:T(2,128)(2,1)} %bitcast.222), kind=kLoop, calls=%fused_computation.2 | loop fusion | flops 1835008 | bytes 3145728 | tf_op jit(solution)/shard_map/reduce_sum | solution.py:186
  250.4 2.1 copy.105
  (40 shorter events, 1.1 us)
Async XLA Ops:
  7.2 50.8 %all-gather.3.cloned.1.call-start = ((), (), s32[]{:S(2)}) async-start(), calls=%async_computation.2 | async-start | bytes 2621440 | tf_op jit(solution)/shard_map/all_gather | solution.py:158
  12.9 47.0 %copy-start.2 = (bf16[1,1,64,8192]{3,2,1,0:T(8,128)(2,1)S(1)}, bf16[1,1,64,8192]{3,2,1,0:T(8,128)(2,1)}, u32[]{:S(2)}) copy-start(bf16[1,1,64,8192]{3,2,1,0:T(8,128)(2,1)} %param.11) | copy-start | bytes 3145732
  76.8 4.7 %copy-start.8 = (s32[1,16,512]{2,1,0:T(8,128)S(1)}, s32[1,16,512]{2,1,0:T(8,128)}, u32[]{:S(2)}) copy-start(s32[1,16,512]{2,1,0:T(8,128)} %param.17) | copy-start | bytes 98308
  76.8 4.8 %copy-start.9 = (s32[1,16,512]{2,1,0:T(8,128)S(1)}, s32[1,16,512]{2,1,0:T(8,128)}, u32[]{:S(2)}) copy-start(s32[1,16,512]{2,1,0:T(8,128)} %param.16) | copy-start | bytes 98308
  76.8 31.1 %all-to-all-start = ((bf16[128,64,128]{2,1,0:T(8,128)(2,1)}), bf16[128,64,128]{2,1,0:T(8,128)(2,1)}, u32[]{:S(2)}, u32[]{:S(2)}) async-start(bf16[128,64,128]{2,1,0:T(8,128)(2,1)} %copy.96), calls=%async_computation | async-start | bytes 4194304 | tf_op jit(solution)/shard_map/all_to_all | solution.py:170
  81.3 66.4 %all-gather.5.cloned.1.call-start = ((), (), s32[]{:S(2)}) async-start(), calls=%async_computation.3 | async-start | bytes 2359296 | tf_op jit(solution)/shard_map/all_gather | solution.py:181
  81.6 1.6 copy-start.11
  87.9 2.7 %copy-start.10 = (s32[1,16,512]{2,1,0:T(8,128)S(1)}, s32[1,16,512]{2,1,0:T(8,128)}, u32[]{:S(2)}) copy-start(s32[1,16,512]{2,1,0:T(8,128)} %param.18) | copy-start | bytes 98308
  87.9 2.7 %copy-start.12 = (f32[1,8]{1,0:T(1,128)S(1)}, f32[1,8]{1,0:T(1,128)}, u32[]{:S(2)}) copy-start(f32[1,8]{1,0:T(1,128)} %param.15) | copy-start | bytes 100
  108.0 2.2 copy-start
  113.8 0.9 copy-start.7
  113.8 2.2 copy-start.1
  114.8 3.7 %copy-start.3 = (f32[1,16,512]{2,1,0:T(8,128)}, f32[1,16,512]{2,1,0:T(8,128)S(1)}, u32[]{:S(2)}) copy-start(f32[1,16,512]{2,1,0:T(8,128)S(1)} %get-tuple-element.13) | copy-start | bytes 98308
  114.8 3.7 %copy-start.5 = (f32[1,16,512]{2,1,0:T(8,128)}, f32[1,16,512]{2,1,0:T(8,128)S(1)}, u32[]{:S(2)}) copy-start(f32[1,16,512]{2,1,0:T(8,128)S(1)} %get-tuple-element.14) | copy-start | bytes 98308
  185.8 4.7 %copy-start.4 = (f32[1,16,512]{2,1,0:T(8,128)S(1)}, f32[1,16,512]{2,1,0:T(8,128)}, u32[]{:S(2)}) copy-start(f32[1,16,512]{2,1,0:T(8,128)} %copy-done.3) | copy-start | bytes 98308
  185.8 4.7 %copy-start.6 = (f32[1,16,512]{2,1,0:T(8,128)S(1)}, f32[1,16,512]{2,1,0:T(8,128)}, u32[]{:S(2)}) copy-start(f32[1,16,512]{2,1,0:T(8,128)} %copy-done.5) | copy-start | bytes 98308
  185.8 53.3 %all-to-all-start.1 = ((bf16[4,2,131072]{2,1,0:T(2,128)(2,1)}), bf16[4,2,131072]{2,1,0:T(2,128)(2,1)S(1)}, u32[]{:S(2)}, u32[]{:S(2)}) async-start(bf16[4,2,131072]{2,1,0:T(2,128)(2,1)} %reshape.702), calls=%async_computation.1 | async-start | bytes 4194304 | tf_op jit(solution)/shard_map/all_to_all | solution.py:185
Sparse Core Ops, SparseCore 0:
  9.5 48.3 all-gather.2
  122.8 24.9 all-gather.4
where the time goes:
time: 260 us; the launch traced here: 259 us
  waiting for transfers between devices  136 us (52%)
  other arithmetic  47.9 us (18%)
  local copies, waits for them, and re-layouts  38.4 us (15%)
  between operations  15.1 us (6%)
  matrix products  12.7 us (5%)
  starting transfers between devices  9.47 us (4%)
    all_to_all x1, waiting for transfers between devices, local(): lax.all_to_all(term[None], 'layer', split_axis=3, concat_axis=0, tiled=True)  47.9 us
    all_gather x1, waiting for transfers between devices, local(): strip_data = lax.all_gather(model_strip, 'layer', axis=3, tiled=True)[0]  45 us
    all_gather x1, waiting for transfers between devices, local(): all_grids = lax.all_gather(adjoint, 'facet', axis=0, tiled=True)  25.1 us
    all_to_all x1, waiting for transfers between devices, local(): lax.all_to_all(contrib, 'facet', split_axis=0, concat_axis=0, tiled=True)  17 us
    unnamed x34, local copies, waits for them, and re-layouts  16.6 us
    unnamed x2, other arithmetic  9.45 us
    add x1, other arithmetic, backward(): image_real * cosine + image_imag * sine_part  8.78 us
    reduce_sum x1, other arithmetic, local(): gradient = jnp.sum(pieces.astype(jnp.float32), axis=0)[None]  7.26 us
  transfers between devices with their start and end apart: 4, of which 4 were waited for; matrix products, arithmetic and copies ran while one was open for 6% of the time, Pallas kernels for 0%

commit v1 on v0

v1 whole, which is shorter than its diff:
```python
import functools
import math

import jax
import jax.numpy as jnp
import numpy as np
from jax import lax
from jax.experimental import pallas as pl
from jax.experimental.pallas import tpu as pltpu
from jax.sharding import PartitionSpec as P

MESH = pl.DeviceIdType.MESH
BACK_GAIN = 8.0
CHUNKS = 8


def _fit(values, degree):
    nodes = np.cos(np.pi * (np.arange(64) + 0.5) / 64)
    y = (nodes + 1.0) * 0.5 * np.pi**2
    cheb = np.polynomial.chebyshev.Chebyshev.fit(y, values(np.sqrt(y)), degree, domain=[0, np.pi**2])
    return [float(v) for v in cheb.convert(kind=np.polynomial.Polynomial).coef]


COS = _fit(np.cos, 8)
SIN = _fit(lambda x: np.sinc(x / np.pi), 7)


def cos_sin(x):
    y = x * x
    c = jnp.full_like(y, COS[-1])
    for v in COS[-2::-1]:
        c = c * y + v
    s = jnp.full_like(y, SIN[-1])
    for v in SIN[-2::-1]:
        s = s * y + v
    return c, s * x


def dft(length):
    k = np.arange(length)
    angles = 2.0 * np.pi * ((k[:, None] * k[None, :]) % length) / length
    scale = 1.0 / math.sqrt(length)
    return np.cos(angles) * scale, -np.sin(angles) * scale


def barrier_line(i, n):
    sem = pltpu.get_barrier_semaphore()

    @pl.when(i > 0)
    def _():
        pl.semaphore_signal(sem, inc=1, device_id={"layer": i - 1}, device_id_type=MESH)

    @pl.when(i < n - 1)
    def _():
        pl.semaphore_signal(sem, inc=1, device_id={"layer": i + 1}, device_id_type=MESH)

    peers = jnp.where(i > 0, 1, 0) + jnp.where(i < n - 1, 1, 0)
    pl.semaphore_wait(sem, peers)


def forward_kernel(n, x_ref, ang_ref, f1_ref, g_ref, tw_ref, fac_ref, out_ref, buf, send_sem, recv_sem, own_sem):
    i = lax.axis_index("layer")
    cq = x_ref.shape[0] // CHUNKS
    subgrids = g_ref.shape[0] // 2
    rows = f1_ref.shape[0] // 2
    barrier_line(i, n)
    own = pltpu.make_async_copy(x_ref, buf.at[i], own_sem)
    own.start()

    def copy(direction, s, q):
        step = 1 if direction == 0 else -1
        origin = jnp.clip(i - step * s, 0, n - 1)
        cols = pl.ds(q * cq, cq)
        src = x_ref.at[cols] if s == 0 else buf.at[origin, cols]
        return pltpu.make_async_remote_copy(
            src_ref=src,
            dst_ref=buf.at[origin, cols],
            send_sem=send_sem.at[direction, s, q],
            recv_sem=recv_sem.at[direction, s, q],
            device_id={"layer": jnp.clip(i + step, 0, n - 1)},
            device_id_type=MESH,
        )

    def sends(direction, s):
        if direction == 0:
            return (i - s >= 0) & (i < n - 1)
        return (i + s <= n - 1) & (i > 0)

    def gets(direction, s):
        return i - 1 - s >= 0 if direction == 0 else i + 1 + s <= n - 1

    def compute(q):
        twr, twi = tw_ref[0], tw_ref[1]
        facr, faci = fac_ref[0], fac_ref[1]
        for pair in range(cq // 2):
            halves = []
            for c in (2 * pair, 2 * pair + 1):
                col = q * cq + c
                xr = jnp.concatenate([buf[l, col, 0] for l in range(n)], axis=0).astype(jnp.float32)
                xi = jnp.concatenate([buf[l, col, 1] for l in range(n)], axis=0).astype(jnp.float32)
                cosine, sine = cos_sin(ang_ref[col].astype(jnp.float32))
                x = jnp.concatenate([xr * cosine - xi * sine, xr * sine + xi * cosine], axis=0)
                h = jnp.dot(f1_ref[...], x.astype(jnp.bfloat16), preferred_element_type=jnp.float32)
                hr, hi = h[:rows], h[rows:]
                halves.append(
                    jnp.concatenate([hr * twr - hi * twi, hr * twi + hi * twr], axis=1).astype(jnp.bfloat16)
                )
            both = jnp.concatenate(halves, axis=0)
            spec = lax.dot_general(
                g_ref[...], both, (((1,), (1,)), ((), ())), preferred_element_type=jnp.float32
            )
            sr, si = spec[:subgrids], spec[subgrids:]
            at = q * (cq // 2) + pair
            out_ref[0, at] = (sr * facr - si * faci).astype(jnp.bfloat16)
            out_ref[1, at] = (sr * faci + si * facr).astype(jnp.bfloat16)

    def body(t, carry):
        @pl.when(t < CHUNKS)
        def _():
            for d in range(2):
                @pl.when(sends(d, 0))
                def _():
                    copy(d, 0, t).start()

        for s in range(n - 1):
            q = t - 1 - s
            @pl.when((q >= 0) & (q < CHUNKS))
            def _():
                for d in range(2):
                    @pl.when(gets(d, s))
                    def _():
                        copy(d, s, q).wait_recv()
                        if s + 1 < n - 1:
                            @pl.when(sends(d, s + 1))
                            def _():
                                copy(d, s + 1, q).start()

        @pl.when(t >= n - 1)
        def _():
            compute(t - (n - 1))

        return carry

    own.wait()
    lax.fori_loop(0, CHUNKS + n - 1, body, 0)

    def drain(q, carry):
        for d in range(2):
            for s in range(n - 1):
                @pl.when(sends(d, s))
                def _():
                    copy(d, s, q).wait_send()
        return carry

    lax.fori_loop(0, CHUNKS, drain, 0)


def backward_kernel(n, a_ref, ang_ref, g_ref, f2_ref, tw_ref, fac_ref, out_ref, term, sbuf, rbuf, send_sem, recv_sem):
    i = lax.axis_index("layer")
    cols = ang_ref.shape[0]
    cq = cols // CHUNKS
    fine = g_ref.shape[0] // 2
    rows = ang_ref.shape[1]
    part = rows // n
    barrier_line(i, n)

    def copy(direction, j, q):
        where = pl.ds(q * cq, cq)
        step = 1 if direction == 0 else -1
        return pltpu.make_async_remote_copy(
            src_ref=sbuf.at[direction, j, where],
            dst_ref=rbuf.at[direction, j, where],
            send_sem=send_sem.at[direction, j, q],
            recv_sem=recv_sem.at[direction, j, q],
            device_id={"layer": jnp.clip(i + step, 0, n - 1)},
            device_id_type=MESH,
        )

    def behind(direction):
        return i > 0 if direction == 0 else i < n - 1

    def compute(q):
        twr, twi = tw_ref[0], tw_ref[1]
        facr, faci = fac_ref[0], fac_ref[1]
        for pair in range(cq // 2):
            at = q * (cq // 2) + pair
            ar = a_ref[0, at].astype(jnp.float32)
            ai = a_ref[1, at].astype(jnp.float32)
            b = jnp.concatenate([ar * facr + ai * faci, ai * facr - ar * faci], axis=0).astype(jnp.bfloat16)
            h = jnp.dot(g_ref[...], b, preferred_element_type=jnp.float32)
            hr, hi = h[:fine], h[fine:]
            mixed = jnp.concatenate([hr * twr + hi * twi, hi * twr - hr * twi], axis=1).astype(jnp.bfloat16)
            image = lax.dot_general(
                f2_ref[...], mixed, (((1,), (1,)), ((), ())), preferred_element_type=jnp.float32
            )
            for c in range(2):
                col = q * cq + 2 * pair + c
                ir = image[2 * c * rows : (2 * c + 1) * rows]
                ii = image[(2 * c + 1) * rows : (2 * c + 2) * rows]
                cosine, sine = cos_sin(ang_ref[col].astype(jnp.float32))
                tr = (BACK_GAIN * (ir * cosine + ii * sine)).astype(jnp.bfloat16)
                ti = (BACK_GAIN * (ii * cosine - ir * sine)).astype(jnp.bfloat16)
                for l in range(n):
                    term[l, col, 0] = tr[l * part : (l + 1) * part]
                    term[l, col, 1] = ti[l * part : (l + 1) * part]

    def relay(direction, j, q):
        where = pl.ds(q * cq, cq)

        @pl.when(behind(direction))
        def _():
            copy(direction, j, q).wait_recv()
            total = term[j, where].astype(jnp.float32) + rbuf[direction, j, where].astype(jnp.float32)
            sbuf[direction, j, where] = total.astype(jnp.bfloat16)

        @pl.when(jnp.logical_not(behind(direction)))
        def _():
            sbuf[direction, j, where] = term[j, where]

        copy(direction, j, q).start()

    def body(t, carry):
        @pl.when(t < CHUNKS)
        def _():
            compute(t)

        for direction in range(2):
            q = t - i if direction == 0 else t - (n - 1 - i)

            @pl.when((q >= 0) & (q < CHUNKS))
            def _():
                for d in range(n - 1, 0, -1):
                    j = i + d if direction == 0 else i - d

                    @pl.when((j < n) & (j >= 0))
                    def _():
                        relay(direction, j, q)

        last = t - (n - 1)

        @pl.when(last >= 0)
        def _():
            where = pl.ds(last * cq, cq)
            out_ref[where] = term[i, where].astype(jnp.float32)
            for direction in range(2):
                @pl.when(behind(direction))
                def _():
                    copy(direction, i, last).wait_recv()
                    out_ref[where] += rbuf[direction, i, where].astype(jnp.float32)

        return carry

    lax.fori_loop(0, CHUNKS + n - 1, body, 0)

    def drain(q, carry):
        for direction in range(2):
            for d in range(1, n):
                j = i + d if direction == 0 else i - d

                @pl.when((j < n) & (j >= 0))
                def _():
                    copy(direction, j, q).wait_send()
        return carry

    lax.fori_loop(0, CHUNKS, drain, 0)


def facet_factor(window, shift_cells, subgrids):
    length = window.shape[0]
    positions = jnp.arange(length, dtype=jnp.int32)
    turn_count = positions * shift_cells % length
    angles = 2.0 * math.pi / length * turn_count.astype(jnp.float32)
    both = jnp.stack([window * jnp.cos(angles), -window * jnp.sin(angles)]).reshape(2, subgrids, -1)
    return jnp.concatenate([both, both], axis=2)


def spread(cells, length, taps):
    count = taps.shape[0]
    lanes = jnp.arange(length, dtype=jnp.int32)
    offset = (lanes - cells[..., None] + (count // 2 + length)) % length
    out = jnp.zeros(offset.shape, jnp.float32)
    for t in range(count):
        out = out + jnp.where(offset == t, taps[t], 0.0)
    return out


def middle(grids, u, v, plane, observed, angle, taps, rows, cols):
    row_weights = spread(u, rows, taps)
    column_weights = spread(v, cols, taps).astype(jnp.bfloat16)
    picked = jnp.einsum("sjc,sck->sjk", column_weights, grids.astype(jnp.bfloat16), preferred_element_type=jnp.float32)
    model_real = jnp.sum(picked[..., :rows] * row_weights, axis=2)
    model_imag = jnp.sum(picked[..., rows:] * row_weights, axis=2)
    pick = plane[..., None] == jnp.arange(angle.shape[0], dtype=jnp.int32)
    cosine = jnp.sum(jnp.where(pick, jnp.cos(angle), 0.0), axis=2)
    sine = jnp.sum(jnp.where(pick, jnp.sin(angle), 0.0), axis=2)
    res_real = observed[:, 0] - (model_real * cosine - model_imag * sine)
    res_imag = observed[:, 1] - (model_real * sine + model_imag * cosine)
    w_real = res_real * cosine + res_imag * sine
    w_imag = res_imag * cosine - res_real * sine
    spread_rows = jnp.concatenate(
        [w_real[..., None] * row_weights, w_imag[..., None] * row_weights], axis=2
    ).astype(jnp.bfloat16)
    adjoint = jnp.einsum("sjc,sjk->sck", column_weights, spread_rows, preferred_element_type=jnp.float32)
    return jnp.stack([res_real, res_imag], axis=1), adjoint.astype(jnp.bfloat16)


def local(n, nf, model_strip, screen_angle, facet_window, facet_shift, kernel_taps, plane_angle, u_cell, v_cell, w_plane, observed):
    _, _, cols, length = screen_angle.shape
    per = u_cell.shape[1]
    subgrids = per * nf
    rows = length // subgrids
    block = rows // n
    vmem = pl.BlockSpec(memory_space=pltpu.VMEM)
    fr, fi = dft(rows)
    gr, gi = dft(subgrids)
    turn = 2.0 * np.pi * (np.arange(rows)[:, None] * np.arange(subgrids)[None, :] % length) / length
    twist = np.stack([np.cos(turn), -np.sin(turn)]).astype(np.float32)
    bf = lambda a: jnp.asarray(a.astype(np.float32)).astype(jnp.bfloat16)
    f1 = bf(np.block([[fr, -fi], [fi, fr]]))
    g1 = bf(np.block([[gr, -gi], [gi, gr]]))
    g2 = bf(np.block([[gr.T, gi.T], [-gi.T, gr.T]]))
    zero = np.zeros_like(fr)
    f2 = bf(
        np.block(
            [
                [fr.T, zero, fi.T, zero],
                [-fi.T, zero, fr.T, zero],
                [zero, fr.T, zero, fi.T],
                [zero, -fi.T, zero, fr.T],
            ]
        )
    )
    tw2 = np.ascontiguousarray(np.tile(np.swapaxes(twist, 1, 2), (1, 1, 2)))
    factor = facet_factor(facet_window[0], facet_shift[0], subgrids)
    x = model_strip[0].reshape(2, cols, block, subgrids).transpose(1, 0, 2, 3)
    angle = screen_angle[0, 0].reshape(cols, rows, subgrids)
    contrib = pl.pallas_call(
        functools.partial(forward_kernel, n),
        out_shape=jax.ShapeDtypeStruct((2, cols // 2, subgrids, 2 * rows), jnp.bfloat16),
        in_specs=[vmem] * 6,
        out_specs=vmem,
        scratch_shapes=[
            pltpu.VMEM((n, cols, 2, block, subgrids), jnp.bfloat16),
            pltpu.SemaphoreType.DMA((2, n - 1, CHUNKS)),
            pltpu.SemaphoreType.DMA((2, n - 1, CHUNKS)),
            pltpu.SemaphoreType.DMA,
        ],
        compiler_params=pltpu.CompilerParams(collective_id=0, has_side_effects=True),
        name="gather_forward",
    )(x, angle, f1, g1, jnp.asarray(twist), factor)
    parts = contrib.reshape(2, cols // 2, nf, per, 2 * rows)
    received = lax.all_to_all(parts, "facet", split_axis=2, concat_axis=2, tiled=True)
    grids = jnp.sum(received.astype(jnp.float32), axis=2)
    grids = grids.reshape(2, cols // 2, per, 2, rows).transpose(2, 1, 3, 0, 4).reshape(per, cols, 2 * rows)
    residual, adjoint = middle(
        grids, u_cell[0], v_cell[0], w_plane[0], observed[0], plane_angle[0], kernel_taps, rows, cols
    )
    adjoint = adjoint.reshape(per, cols // 2, 2, 2, rows).transpose(3, 1, 0, 2, 4).reshape(2, cols // 2, per, 2 * rows)
    every = lax.all_gather(adjoint, "facet", axis=2, tiled=True)
    gradient = pl.pallas_call(
        functools.partial(backward_kernel, n),
        out_shape=jax.ShapeDtypeStruct((cols, 2, block, subgrids), jnp.float32),
        in_specs=[vmem] * 6,
        out_specs=vmem,
        scratch_shapes=[
            pltpu.VMEM((n, cols, 2, block, subgrids), jnp.bfloat16),
            pltpu.VMEM((2, n, cols, 2, block, subgrids), jnp.bfloat16),
            pltpu.VMEM((2, n, cols, 2, block, subgrids), jnp.bfloat16),
            pltpu.SemaphoreType.DMA((2, n, CHUNKS)),
            pltpu.SemaphoreType.DMA((2, n, CHUNKS)),
        ],
        compiler_params=pltpu.CompilerParams(collective_id=1, has_side_effects=True),
        name="backward_scatter",
    )(every, angle, g2, f2, jnp.asarray(tw2), factor)
    gradient = gradient.transpose(1, 0, 2, 3).reshape(1, 2, cols, block * subgrids)
    return (residual[None], gradient)


def solution(mesh):
    return jax.shard_map(
        functools.partial(local, mesh.shape["layer"], mesh.shape["facet"]),
        mesh=mesh,
        in_specs=(
            P("facet", None, None, "layer"),
            P("layer", "facet", None, None),
            P("facet", None),
            P("facet"),
            P(),
            P("layer", None),
            P("layer", "facet", None),
            P("layer", "facet", None),
            P("layer", "facet", None),
            P("layer", "facet", None, None),
        ),
        out_specs=(P("layer", "facet", None, None), P("facet", None, None, "layer")),
        check_vma=False,
    )
```

time: 260 us -> 207 us (0.80)
  Pallas kernels: 0 us -> 90.9 us
  waiting for transfers between devices: 136 us -> 50.8 us
  other arithmetic: 47.9 us -> 17.3 us
  local copies, waits for them, and re-layouts: 38.4 us -> 14.7 us
  starting transfers between devices: 9.47 us -> 3.9 us
    pallas_call x0 -> x2, Pallas kernels: none -> 90.9 us  [the longest x1 47 us: local(): pl.pallas_call(functools.partial(backward_kernel, n), out_shape=jax.Shape...]
    all_gather x2 -> x1, waiting for transfers between devices: 70.1 us -> 25.2 us  [local(): every = lax.all_gather(adjoint, 'facet', axis=2, tiled=True)]
    all_to_all x2 -> x1, waiting for transfers between devices: 64.9 us -> 25.6 us  [local(): lax.all_to_all(parts, 'facet', split_axis=2, concat_axis=2, tiled=True)]
    unnamed x34 -> x19, local copies, waits for them, and re-layouts: 16.6 us -> 4.9 us
    unnamed x2 -> x0, other arithmetic: 9.45 us -> none
    add x2 -> x1, other arithmetic: 8.81 us -> 0.02 us  [middle(): w_real = res_real * cosine + res_imag * sine]
    reduce_sum x5 -> x3, other arithmetic: 15.1 us -> 7.59 us  [the longest x1 6.98 us: middle(): model_real = jnp.sum(picked[..., :rows] * row_weights, axis=2)]
    reshape x0 -> x5, local copies, waits for them, and re-layouts: none -> 6.78 us  [the longest x1 3.49 us: local(): parts = contrib.reshape(2, cols // 2, nf, per, 2 * rows)]
  transfers between devices with their start and end apart: 4 -> 2, of which waited for: 4 -> 2; matrix products, arithmetic and copies ran while one was open for 6% -> 1% of each run, Pallas kernels for 0% -> 0%
where the time goes in v1:
time: 207 us; the launch traced here: 206 us
  Pallas kernels  90.9 us (44%)
  waiting for transfers between devices  50.8 us (25%)
  other arithmetic  17.3 us (8%)
  between operations  14.9 us (7%)
  local copies, waits for them, and re-layouts  14.7 us (7%)
  matrix products  13.8 us (7%)
  starting transfers between devices  3.9 us (2%)
    pallas_call x1, Pallas kernels, local(): pl.pallas_call(functools.partial(backward_kernel, n), out_shape=jax.Shape...  47 us
    pallas_call x1, Pallas kernels, local(): pl.pallas_call(functools.partial(forward_kernel, n), out_shape=jax.ShapeD...  43.9 us
    all_to_all x1, waiting for transfers between devices, local(): lax.all_to_all(parts, 'facet', split_axis=2, concat_axis=2, tiled=True)  25.6 us
    all_gather x1, waiting for transfers between devices, local(): every = lax.all_gather(adjoint, 'facet', axis=2, tiled=True)  25.2 us
    dot_general x1, matrix products, middle(): jnp.einsum('sjc,sck->sjk', column_weights, grids.astype(jnp.bfloat16), pr...  7.01 us
    reduce_sum x1, other arithmetic, middle(): model_real = jnp.sum(picked[..., :rows] * row_weights, axis=2)  6.98 us
    dot_general x1, matrix products, middle(): jnp.einsum('sjc,sjk->sck', column_weights, spread_rows, preferred_element...  6.83 us
    another operation x1, other arithmetic  6.83 us
  transfers between devices with their start and end apart: 2, of which 2 were waited for; matrix products, arithmetic and copies ran while one was open for 1% of the time, Pallas kernels for 0%

profile of v1, /device:TPU:0, one launch (start us, length us, event | category | flops | bytes accessed | tf_op | source)
XLA Modules:
  0.0 206.4 jit_solution(6555976414474144815)
XLA Ops:
  7.2 0.0 copy-start
  7.9 2.1 %multiply_reduce_fusion.1 = (f32[8192]{0:T(1024)S(1)}, f32[8192]{0:T(1024)S(1)}) fusion(f32[1,8192]{1,0:T(1,128)} %param.18, s32[]{:T(128)} %bitcast.64), kind=kLoop, calls=%fused_computation.45 | loop fusion | flops 139264 | bytes 98308 | tf_op jit(solution)/shard_map/mul | solution.py:273
  10.0 0.1 stack.14
  10.1 0.1 stack.15
  10.1 2.5 %copy.60 = bf16[8,8,64,128]{3,2,1,0:T(8,128)(2,1)} copy(bf16[8,8,64,128]{3,1,2,0:T(8,128)(2,1)} %bitcast.72) | data formatting | bytes 2097152
  12.6 0.0 copy-done
  12.6 0.1 copy.59
  12.7 0.8 copy_bitcast_fusion.x_ref
  13.6 0.7 maximum_maximum_fusion.fac_ref
  14.3 43.9 %gather_forward.1 = bf16[2,32,128,128]{3,2,1,0:T(8,128)(2,1)} custom-call(bf16[64,2,16,128]{3,2,1,0:T(8,128)(2,1)} %copy_bitcast_fusion.x_ref, bf16[64,64,128]{2,1,0:T(8,128)(2,1)} %bitcast.65, bf16[128,128]{1,0:T(8,128)(2,1)} %constant.82.f1_ref, bf16[256,256]{1,0:T(8,128)(2,1)} %constant.83.g_ref, f32[2,64,128]{2,1,0:T(8,128)} %constant.71.clone.tw_ref, ...), custom_call_target="tpu_custom_call" | custom-call | tf_op jit(solution)/shard_map/gather_forward/pallas_call | solution.py:337
  58.3 3.5 %copy.51 = bf16[2,32,8,16,128]{4,3,1,0,2:T(8,128)(2,1)} copy(bf16[2,32,8,16,128]{4,3,2,1,0:T(8,128)(2,1)} %bitcast.67) | data formatting | bytes 4194304 | tf_op jit(solution)/shard_map/reshape | solution.py:351
  61.8 0.0 copy-start.2
  61.8 0.0 copy-start.4
  61.8 0.0 copy-start.6
  61.8 0.0 copy-start.3
  61.8 3.9 %all-to-all-start = ((bf16[2,32,8,16,128]{4,3,1,0,2:T(8,128)(2,1)}), bf16[2,32,8,16,128]{4,3,1,0,2:T(8,128)(2,1)S(1)}, u32[]{:S(2)}, u32[]{:S(2)}) async-start(bf16[2,32,8,16,128]{4,3,1,0,2:T(8,128)(2,1)} %copy.51), calls=%async_computation | async-start | bytes 4194304 | tf_op jit(solution)/shard_map/all_to_all | solution.py:352
  65.6 0.0 all-gather.2.cloned.1.call-start
  65.7 0.0 copy-done.2
  65.7 0.0 copy-done.4
  65.7 0.6 fusion.38
  66.4 0.0 copy-done.6
  66.4 0.0 copy-done.3
  66.4 0.2 select_reduce_fusion
  66.6 0.0 copy-start.5
  66.6 25.6 %all-to-all-done = bf16[2,32,8,16,128]{4,3,1,0,2:T(8,128)(2,1)S(1)} async-done(((bf16[2,32,8,16,128]{4,3,1,0,2:T(8,128)(2,1)}), bf16[2,32,8,16,128]{4,3,1,0,2:T(8,128)(2,1)S(1)}, u32[]{:S(2)}, u32[]{:S(2)}) %all-to-all-start) | async-done | bytes 2097184 | tf_op jit(solution)/shard_map/all_to_all | solution.py:352
  92.2 0.4 reduce_sum.48
  92.6 0.2 convert_element_type.48
  92.9 0.8 copy.52
  93.7 0.2 convert_element_type.50
  94.0 0.0 copy-done.5
  94.0 0.0 copy-start.1
  94.0 7.0 %fusion.11 = f32[16,512,128]{1,2,0:T(8,128)S(1)} fusion(bf16[16,64,128]{2,1,0:T(8,128)(2,1)S(1)} %convert_element_type.50, f32[]{:T(128)} %bitcast.8, f32[]{:T(128)} %bitcast.7, f32[]{:T(128)} %bitcast.6, f32[]{:T(128)} %bitcast.5, f32[]{:T(128)} %bitcast.4, f32[]{:T(128)} %bitcast.3, f32[]{:T(128)} %bitcast.2, s32[16,512]{1,0:T(8,128)S(1)} %bitcast.79), kind=kOutput, calls=%fused_computation.21 | convolution fusion | flops 152043520 | bytes 4489244 | tf_op jit(solution)/shard_map/sjc,sck->sjk/dot_general | solution.py:290
  101.0 0.0 copy-done.1
  101.0 7.0 %fusion.3 = (f32[16,512]{1,0:T(8,128)S(1)}, f32[16,512]{1,0:T(8,128)S(1)}) fusion(f32[16,512,128]{1,2,0:T(8,128)S(1)} %fusion.11, f32[]{:T(128)} %bitcast.8, f32[]{:T(128)} %bitcast.7, f32[]{:T(128)} %bitcast.6, f32[]{:T(128)} %bitcast.5, f32[]{:T(128)} %bitcast.4, f32[]{:T(128)} %bitcast.3, f32[]{:T(128)} %bitcast.2, s32[16,512]{1,0:T(8,128)S(1)} %bitcast.76), kind=kLoop, calls=%fused_computation.11 | loop fusion | flops 19382272 | bytes 4292636 | tf_op jit(solution)/shard_map/reduce_sum | solution.py:291
  108.0 6.8 %multiply_convert_fusion.1 = (bf16[16,512,64]{1,2,0:T(8,128)(2,1)S(1)}, bf16[16,512,64]{1,2,0:T(8,128)(2,1)S(1)}) fusion(f32[16,512]{1,0:T(8,128)S(1)} %get-tuple-element.18, f32[]{:T(128)} %bitcast.8, f32[]{:T(128)} %bitcast.7, f32[]{:T(128)} %bitcast.6, f32[]{:T(128)} %bitcast.5, f32[]{:T(128)} %bitcast.4, f32[]{:T(128)} %bitcast.3, f32[]{:T(128)} %bitcast.2, ...), kind=kLoop, calls=%fused_computation.17 | loop fusion | flops 19398656 | bytes 2195484 | tf_op jit(solution)/shard_map/convert.1
  114.9 6.8 %fusion.8 = bf16[16,64,128]{2,1,0:T(8,128)(2,1)S(1)} fusion(bf16[16,512,64]{1,2,0:T(8,128)(2,1)S(1)} %get-tuple-element.23, bf16[16,512,64]{1,2,0:T(8,128)(2,1)S(1)} %get-tuple-element.22, f32[]{:T(128)} %bitcast.8, f32[]{:T(128)} %bitcast.7, f32[]{:T(128)} %bitcast.6, f32[]{:T(128)} %bitcast.5, f32[]{:T(128)} %bitcast.4, f32[]{:T(128)} %bitcast.3, ...), kind=kOutput, calls=%fused_computation.20 | convolution fusion | flops 156368896 | bytes 2392092 | tf_op jit(solution)/shard_map/sjc,sjk->sck/dot_general | solution.py:303
  121.7 0.2 reshape.182
  122.0 0.3 copy.64
  122.3 1.0 reshape.183
  123.2 0.0 all-gather.2.cloned.1.call-update
  123.3 0.7 copy.55
  124.0 25.2 %all-gather.2.cloned.1.call-done.a_ref = bf16[2,32,128,128]{3,2,1,0:T(8,128)(2,1)} async-done(((bf16[2,32,16,128]{3,2,1,0:T(8,128)(2,1)}), bf16[2,32,128,128]{3,2,1,0:T(8,128)(2,1)}) %all-gather.2.cloned.1.call-update) | async-done | bytes 2097168 | tf_op jit(solution)/shard_map/all_gather | solution.py:359
  149.2 47.0 %backward_scatter.1 = f32[64,2,16,128]{3,2,1,0:T(8,128)} custom-call(bf16[2,32,128,128]{3,2,1,0:T(8,128)(2,1)} %all-gather.2.cloned.1.call-done.a_ref, bf16[64,64,128]{2,1,0:T(8,128)(2,1)} %bitcast.66, bf16[256,256]{1,0:T(8,128)(2,1)} %constant.84.g_ref, bf16[256,256]{1,0:T(8,128)(2,1)} %constant.85.f2_ref, f32[2,128,128]{2,1,0:T(8,128)} %constant.72.clone.tw_ref, ...), custom_call_target="tpu_custom_call" | custom-call | tf_op jit(solution)/shard_map/backward_scatter/pallas_call | solution.py:360
  196.2 1.8 reshape.184
  198.0 1.6 copy.56
  (5 shorter events, 0.1 us)
Async XLA Ops:
  7.2 5.5 %copy-start = (bf16[1,2,64,2048]{3,2,1,0:T(8,128)(2,1)S(1)}, bf16[1,2,64,2048]{3,2,1,0:T(8,128)(2,1)}, u32[]{:S(2)}) copy-start(bf16[1,2,64,2048]{3,2,1,0:T(8,128)(2,1)} %param.16) | copy-start | bytes 1572868
  61.8 3.9 %copy-start.2 = (f32[1,16,2,512]{3,2,1,0:T(2,128)S(1)}, f32[1,16,2,512]{3,2,1,0:T(2,128)}, u32[]{:S(2)}) copy-start(f32[1,16,2,512]{3,2,1,0:T(2,128)} %param.25) | copy-start | bytes 196612
  61.8 4.0 %copy-start.4 = (f32[7]{0:T(128)S(1)}, f32[7]{0:T(128)}, u32[]{:S(2)}) copy-start(f32[7]{0:T(128)} %param.20) | copy-start | bytes 88
  61.8 4.6 %copy-start.6 = (f32[1,8]{1,0:T(1,128)S(1)}, f32[1,8]{1,0:T(1,128)}, u32[]{:S(2)}) copy-start(f32[1,8]{1,0:T(1,128)} %param.21) | copy-start | bytes 100
  61.8 4.6 %copy-start.3 = (s32[1,16,512]{2,1,0:T(8,128)S(1)}, s32[1,16,512]{2,1,0:T(8,128)}, u32[]{:S(2)}) copy-start(s32[1,16,512]{2,1,0:T(8,128)} %param.24) | copy-start | bytes 98308
  61.8 30.5 %all-to-all-start = ((bf16[2,32,8,16,128]{4,3,1,0,2:T(8,128)(2,1)}), bf16[2,32,8,16,128]{4,3,1,0,2:T(8,128)(2,1)S(1)}, u32[]{:S(2)}, u32[]{:S(2)}) async-start(bf16[2,32,8,16,128]{4,3,1,0,2:T(8,128)(2,1)} %copy.51), calls=%async_computation | async-start | bytes 4194304 | tf_op jit(solution)/shard_map/all_to_all | solution.py:352
  65.6 83.6 %all-gather.2.cloned.1.call-start = ((), (), s32[]{:S(2)}) async-start(), calls=%async_computation.1 | async-start | bytes 2359296 | tf_op jit(solution)/shard_map/all_gather | solution.py:359
  66.6 27.3 %copy-start.5 = (s32[1,16,512]{2,1,0:T(8,128)S(1)}, s32[1,16,512]{2,1,0:T(8,128)}, u32[]{:S(2)}) copy-start(s32[1,16,512]{2,1,0:T(8,128)} %param.23) | copy-start | bytes 98308
  94.0 7.0 %copy-start.1 = (s32[1,16,512]{2,1,0:T(8,128)S(1)}, s32[1,16,512]{2,1,0:T(8,128)}, u32[]{:S(2)}) copy-start(s32[1,16,512]{2,1,0:T(8,128)} %param.22) | copy-start | bytes 98308
Sparse Core Ops, SparseCore 0:
  123.4 25.7 all-gather.1

commit v2 on v1

--- a/solution.py
+++ b/solution.py
@@ -304,6 +304,205 @@
     return jnp.stack([res_real, res_imag], axis=1), adjoint.astype(jnp.bfloat16)
 
 
+def middle_kernel(
+    contrib_ref, u_ref, v_ref, plane_ref, obs_ref, taps_ref, table_ref, res_ref, out_ref,
+    r0, acc0, r1, acc1, r2, fin, adj, phase, s0, d0, s1, d1, s2, d2, sg, dg,
+):
+    pairs = contrib_ref.shape[1]
+    per, vis = u_ref.shape
+    rows = contrib_ref.shape[3] // 2
+    cols = 2 * pairs
+    f = lax.axis_index("facet")
+    core = lax.rem(f, 2)
+    chip = lax.div(f, 2)
+    bits = (lax.rem(chip, 2), lax.div(chip, 2))
+
+    def flip(b):
+        return f + (1 - 2 * bits[b]) * (2 * (1 + b))
+
+    other = f + 1 - 2 * core
+    barrier = pltpu.get_barrier_semaphore()
+    for peer in (other, flip(0), flip(1)):
+        pl.semaphore_signal(barrier, inc=1, device_id={"facet": peer}, device_id_type=MESH)
+    pl.semaphore_wait(barrier, 3)
+
+    def rows_of(device):
+        return pl.ds(pl.multiple_of(device * per, per), per)
+
+    def compose(p, along, across):
+        return along + 2 * across if p == 0 else across + 2 * along
+
+    def remote(src, dst, send, recv, device):
+        return pltpu.make_async_remote_copy(
+            src_ref=src, dst_ref=dst, send_sem=send, recv_sem=recv,
+            device_id={"facet": device}, device_id_type=MESH,
+        )
+
+    def stage0(p, h):
+        return remote(
+            contrib_ref.at[p, :, rows_of(2 * h + 1 - core)], r0.at[p, h], s0.at[p, h], d0.at[p, h], other
+        )
+
+    def stage1(p, k):
+        return remote(acc0.at[p, compose(p, 1 - bits[p], k)], r1.at[p, k], s1.at[p, k], d1.at[p, k], flip(p))
+
+    def stage2(p):
+        return remote(acc1.at[p, 1 - bits[1 - p]], r2.at[p], s2.at[p], d2.at[p], flip(1 - p))
+
+    def add0(p, h):
+        stage0(p, h).wait_recv()
+        mine = contrib_ref[p, :, rows_of(2 * h + core)].astype(jnp.float32)
+        acc0[p, h] = (mine + r0[p, h].astype(jnp.float32)).astype(jnp.bfloat16)
+
+    order = [(a, k, p) for a in (1, 0) for k in range(2) for p in range(2)]
+    for a, k, p in order:
+        stage0(p, compose(p, 1 - bits[p] if a else bits[p], k)).start()
+    for k in range(2):
+        for p in range(2):
+            add0(p, compose(p, 1 - bits[p], k))
+            stage1(p, k).start()
+    for k in range(2):
+        for p in range(2):
+            add0(p, compose(p, bits[p], k))
+
+    plane = plane_ref[...]
+    cosine = jnp.zeros(plane.shape, jnp.float32)
+    sine = jnp.zeros(plane.shape, jnp.float32)
+    for k in range(table_ref.shape[1]):
+        hit = plane == k
+        cosine = jnp.where(hit, table_ref[0, k], cosine)
+        sine = jnp.where(hit, table_ref[1, k], sine)
+    phase[0] = cosine
+    phase[1] = sine
+
+    for k in range(2):
+        for p in range(2):
+            stage1(p, k).wait_recv()
+            total = acc0[p, compose(p, bits[p], k)].astype(jnp.float32) + r1[p, k].astype(jnp.float32)
+            acc1[p, k] = total.astype(jnp.bfloat16)
+    for p in range(2):
+        stage2(p).start()
+    for p in range(2):
+        stage2(p).wait_recv()
+        for t in range(pairs):
+            total = acc1[p, bits[1 - p], t].astype(jnp.float32) + r2[p, t].astype(jnp.float32)
+            fin[p, pl.ds(t, per, stride=pairs), :] = total
+
+    def weights(cells, position, length):
+        count = taps_ref.shape[0]
+        offset = position - cells + count // 2
+        offset = jnp.where(offset < 0, offset + length, jnp.where(offset >= length, offset - length, offset))
+        out = jnp.zeros(offset.shape, jnp.float32)
+        for t in range(count):
+            out = jnp.where(offset == t, taps_ref[t], out)
+        return out
+
+    def one(s, carry):
+        at = pl.ds(s, 1)
+        where = pl.ds(pl.multiple_of(s * pairs, pairs), pairs)
+        row = lax.broadcasted_iota(jnp.int32, (rows, vis), 0)
+        half = lax.broadcasted_iota(jnp.int32, (pairs, vis), 0)
+        col = jnp.concatenate([2 * half, 2 * half + 1], axis=0)
+        row_weights = weights(u_ref[at, :], row, rows)
+        column_weights = weights(v_ref[at, :], col, cols).astype(jnp.bfloat16)
+        real, imag = fin[0, where, :], fin[1, where, :]
+        grid = jnp.concatenate(
+            [
+                jnp.concatenate([real[:, :rows], imag[:, :rows]], axis=1),
+                jnp.concatenate([real[:, rows:], imag[:, rows:]], axis=1),
+            ],
+            axis=0,
+        )
+        picked = lax.dot_general(
+            grid.astype(jnp.bfloat16), column_weights, (((0,), (0,)), ((), ())),
+            preferred_element_type=jnp.float32,
+        )
+        model_real = jnp.sum(picked[:rows] * row_weights, axis=0, keepdims=True)
+        model_imag = jnp.sum(picked[rows:] * row_weights, axis=0, keepdims=True)
+        cosine, sine = phase[0, at, :], phase[1, at, :]
+        res_real = obs_ref[s, 0:1, :] - (model_real * cosine - model_imag * sine)
+        res_imag = obs_ref[s, 1:2, :] - (model_real * sine + model_imag * cosine)
+        res_ref[s, 0:1, :] = res_real
+        res_ref[s, 1:2, :] = res_imag
+        w_real = res_real * cosine + res_imag * sine
+        w_imag = res_imag * cosine - res_real * sine
+        spread_rows = jnp.concatenate([row_weights * w_real, row_weights * w_imag], axis=0).astype(jnp.bfloat16)
+        back = lax.dot_general(
+            column_weights, spread_rows, (((1,), (1,)), ((), ())), preferred_element_type=jnp.float32
+        )
+        adj[0, where, :] = jnp.concatenate([back[:pairs, :rows], back[pairs:, :rows]], axis=1)
+        adj[1, where, :] = jnp.concatenate([back[:pairs, rows:], back[pairs:, rows:]], axis=1)
+        return carry
+
+    lax.fori_loop(0, per, one, 0)
+
+    def gather(step, p, device, peer):
+        block = out_ref.at[p, :, rows_of(device)]
+        return remote(block, block, sg.at[step, p, device], dg.at[p, device], peer)
+
+    def far(p, a, k):
+        along = 1 - bits[p] if a else bits[p]
+        across = 1 - bits[1 - p] if k else bits[1 - p]
+        return 2 * compose(p, along, across) + core
+
+    for p in range(2):
+        for t in range(pairs):
+            out_ref[p, t, rows_of(f)] = adj[p, pl.ds(t, per, stride=pairs), :].astype(jnp.bfloat16)
+        gather(0, p, f, flip(1 - p)).start()
+        gather(1, p, f, flip(p)).start()
+        gather(2, p, f, other).start()
+    for p in range(2):
+        block = far(p, 0, 1)
+        gather(0, p, block, flip(1 - p)).wait_recv()
+        gather(1, p, block, flip(p)).start()
+        gather(2, p, block, other).start()
+    for k in range(2):
+        for p in range(2):
+            block = far(p, 1, k)
+            gather(1, p, block, flip(p)).wait_recv()
+            gather(2, p, block, other).start()
+    for p in range(2):
+        for h in range(4):
+            gather(2, p, 2 * h + 1 - core, other).wait_recv()
+    for p in range(2):
+        for h in range(4):
+            stage0(p, h).wait_send()
+            gather(2, p, 2 * h + core, other).wait_send()
+        for k in range(2):
+            stage1(p, k).wait_send()
+            gather(1, p, far(p, 0, k), flip(p)).wait_send()
+        stage2(p).wait_send()
+        gather(0, p, f, flip(1 - p)).wait_send()
+
+
+def fused_middle(contrib, u, v, plane, observed, taps, table):
+    _, pairs, subgrids, lanes = contrib.shape
+    per, vis = u.shape
+    vmem = pl.BlockSpec(memory_space=pltpu.VMEM)
+    smem = pl.BlockSpec(memory_space=pltpu.SMEM)
+    block = (pairs, per, lanes)
+    wire = lambda *lead: pltpu.VMEM((*lead, *block), jnp.bfloat16)
+    dma = lambda *shape: pltpu.SemaphoreType.DMA(shape)
+    return pl.pallas_call(
+        middle_kernel,
+        out_shape=(
+            jax.ShapeDtypeStruct((per, 2, vis), jnp.float32),
+            jax.ShapeDtypeStruct(contrib.shape, jnp.bfloat16),
+        ),
+        in_specs=[vmem] * 5 + [smem] * 2,
+        out_specs=(vmem, vmem),
+        scratch_shapes=[
+            wire(2, 4), wire(2, 4), wire(2, 2), wire(2, 2), wire(2),
+            pltpu.VMEM((2, per * pairs, lanes), jnp.float32),
+            pltpu.VMEM((2, per * pairs, lanes), jnp.float32),
+            pltpu.VMEM((2, per, vis), jnp.float32),
+            dma(2, 4), dma(2, 4), dma(2, 2), dma(2, 2), dma(2), dma(2), dma(3, 2, 8), dma(2, 8),
+        ],
+        compiler_params=pltpu.CompilerParams(collective_id=2, has_side_effects=True),
+        name="degrid_exchange",
+    )(contrib, u, v, plane, observed, taps, table)
+
+
 def local(n, nf, model_strip, screen_angle, facet_window, facet_shift, kernel_taps, plane_angle, u_cell, v_cell, w_plane, observed):
     _, _, cols, length = screen_angle.shape
     per = u_cell.shape[1]
@@ -348,15 +547,21 @@
         compiler_params=pltpu.CompilerParams(collective_id=0, has_side_effects=True),
         name="gather_forward",
     )(x, angle, f1, g1, jnp.asarray(twist), factor)
-    parts = contrib.reshape(2, cols // 2, nf, per, 2 * rows)
-    received = lax.all_to_all(parts, "facet", split_axis=2, concat_axis=2, tiled=True)
-    grids = jnp.sum(received.astype(jnp.float32), axis=2)
-    grids = grids.reshape(2, cols // 2, per, 2, rows).transpose(2, 1, 3, 0, 4).reshape(per, cols, 2 * rows)
-    residual, adjoint = middle(
-        grids, u_cell[0], v_cell[0], w_plane[0], observed[0], plane_angle[0], kernel_taps, rows, cols
-    )
-    adjoint = adjoint.reshape(per, cols // 2, 2, 2, rows).transpose(3, 1, 0, 2, 4).reshape(2, cols // 2, per, 2 * rows)
-    every = lax.all_gather(adjoint, "facet", axis=2, tiled=True)
+    if nf == 8 and per % 16 == 0:
+        table = jnp.stack([jnp.cos(plane_angle[0]), jnp.sin(plane_angle[0])])
+        residual, every = fused_middle(
+            contrib, u_cell[0], v_cell[0], w_plane[0], observed[0], kernel_taps, table
+        )
+    else:
+        parts = contrib.reshape(2, cols // 2, nf, per, 2 * rows)
+        received = lax.all_to_all(parts, "facet", split_axis=2, concat_axis=2, tiled=True)
+        grids = jnp.sum(received.astype(jnp.float32), axis=2)
+        grids = grids.reshape(2, cols // 2, per, 2, rows).transpose(2, 1, 3, 0, 4).reshape(per, cols, 2 * rows)
+        residual, adjoint = middle(
+            grids, u_cell[0], v_cell[0], w_plane[0], observed[0], plane_angle[0], kernel_taps, rows, cols
+        )
+        adjoint = adjoint.reshape(per, cols // 2, 2, 2, rows).transpose(3, 1, 0, 2, 4).reshape(2, cols // 2, per, 2 * rows)
+        every = lax.all_gather(adjoint, "facet", axis=2, tiled=True)
     gradient = pl.pallas_call(
         functools.partial(backward_kernel, n),
         out_shape=jax.ShapeDtypeStruct((cols, 2, block, subgrids), jnp.float32),

time: 207 us -> 144 us (0.70)
  waiting for transfers between devices: 50.8 us -> 0 us
  Pallas kernels: 90.9 us -> 131 us
  other arithmetic: 17.3 us -> 3.43 us
  matrix products: 13.8 us -> 0 us
  between operations: 14.9 us -> 1.43 us
  local copies, waits for them, and re-layouts: 14.7 us -> 8.09 us
  starting transfers between devices: 3.9 us -> 0 us
    pallas_call x0 -> x1, Pallas kernels: none -> 41.6 us  [fused_middle(): pl.pallas_call(middle_kernel, out_shape=(jax.ShapeDtypeStruct((per, 2, vi...]
    all_to_all x1 -> x0, waiting for transfers between devices: 25.6 us -> none  [local(): lax.all_to_all(parts, 'facet', split_axis=2, concat_axis=2, tiled=True)]
    all_gather x1 -> x0, waiting for transfers between devices: 25.2 us -> none  [local(): every = lax.all_gather(adjoint, 'facet', axis=2, tiled=True)]
    dot_general x2 -> x0, matrix products: 13.8 us -> none  [the longest x1 7.01 us: middle(): jnp.einsum('sjc,sck->sjk', column_weights, grids.astype(jnp.bfloat16), pr...]
    reduce_sum x3 -> x0, other arithmetic: 7.59 us -> none  [the longest x1 6.98 us: middle(): model_real = jnp.sum(picked[..., :rows] * row_weights, axis=2)]
    another operation x1, other arithmetic: 6.83 us -> 0.58 us  [local(): table = jnp.stack([jnp.cos(plane_angle[0]), jnp.sin(plane_angle[0])])]
    reshape x4 -> x0, local copies, waits for them, and re-layouts: 5.02 us -> none  [the longest x1 3.49 us: local(): parts = contrib.reshape(2, cols // 2, nf, per, 2 * rows)]
    all_to_all x1 -> x0, starting transfers between devices: 3.87 us -> none  [local(): lax.all_to_all(parts, 'facet', split_axis=2, concat_axis=2, tiled=True)]
  transfers between devices with their start and end apart: 2 -> 0, of which waited for: 2 -> 0; matrix products, arithmetic and copies ran while one was open for 1% -> 0% of each run, Pallas kernels for 0% -> 0%
where the time goes in v2:
time: 144 us
  Pallas kernels  131 us (91%)
  local copies, waits for them, and re-layouts  8.09 us (6%)
  other arithmetic  3.43 us (2%)
    pallas_call x1, Pallas kernels, local(): pl.pallas_call(functools.partial(backward_kernel, n), out_shape=jax.Shape...  45.4 us
    pallas_call x1, Pallas kernels, local(): pl.pallas_call(functools.partial(forward_kernel, n), out_shape=jax.ShapeD...  43.9 us
    pallas_call x1, Pallas kernels, fused_middle(): pl.pallas_call(middle_kernel, out_shape=(jax.ShapeDtypeStruct((per, 2, vi...  41.6 us
    unnamed x8, local copies, waits for them, and re-layouts  4.62 us

profile of v2, /device:TPU:0, one launch (start us, length us, event | category | flops | bytes accessed | tf_op | source)
XLA Modules:
  0.0 143.8 jit_solution(13238904240357618777)
XLA Ops:
  0.6 0.0 copy-start
  1.4 0.7 fusion.3
  2.1 0.6 pad_maximum_fusion.table_ref
  2.6 2.1 %multiply_reduce_fusion.1 = (f32[8192]{0:T(1024)S(1)}, f32[8192]{0:T(1024)S(1)}) fusion(f32[1,8192]{1,0:T(1,128)} %param.18, s32[]{:T(128)} %bitcast.26), kind=kLoop, calls=%fused_computation.9 | loop fusion | flops 139264 | bytes 98308 | tf_op jit(solution)/shard_map/mul | solution.py:273
  4.8 0.1 stack.14
  4.8 0.1 stack.15
  4.9 0.8 maximum_maximum_fusion.fac_ref
  5.7 1.1 copy.23
  6.8 0.8 copy_bitcast_fusion.x_ref
  7.6 0.0 copy-done
  7.6 1.3 copy.24
  8.9 43.9 %gather_forward.1.contrib_ref = bf16[2,32,128,128]{3,2,1,0:T(8,128)(2,1)} custom-call(bf16[64,2,16,128]{3,2,1,0:T(8,128)(2,1)} %copy_bitcast_fusion.x_ref, bf16[64,64,128]{2,1,0:T(8,128)(2,1)} %bitcast.27, bf16[128,128]{1,0:T(8,128)(2,1)} %constant.44.f1_ref, bf16[256,256]{1,0:T(8,128)(2,1)} %constant.45.g_ref, f32[2,64,128]{2,1,0:T(8,128)} %constant.33.clone.tw_ref, ...), custom_call_target="tpu_custom_call" | custom-call | tf_op jit(solution)/shard_map/gather_forward/pallas_call | solution.py:536
  52.8 41.6 %degrid_exchange.1 = (f32[16,2,512]{2,1,0:T(2,128)}, bf16[2,32,128,128]{3,2,1,0:T(8,128)(2,1)}) custom-call(bf16[2,32,128,128]{3,2,1,0:T(8,128)(2,1)} %gather_forward.1.contrib_ref, s32[16,512]{1,0:T(8,128)} %bitcast.35, s32[16,512]{1,0:T(8,128)} %bitcast.36, s32[16,512]{1,0:T(8,128)} %bitcast.37, f32[16,2,512]{2,1,0:T(2,128)} %bitcast.33, f32[7]{0:T(128)} %taps_ref.1, ...), custom_call_target="tpu_custom_call" | custom-call | tf_op jit(solution)/shard_map/degrid_exchange/pallas_call | solution.py:486
  94.4 45.4 %backward_scatter.1 = f32[64,2,16,128]{3,2,1,0:T(8,128)} custom-call(bf16[2,32,128,128]{3,2,1,0:T(8,128)(2,1)} %get-tuple-element.5.a_ref, bf16[64,64,128]{2,1,0:T(8,128)(2,1)} %bitcast.28, bf16[256,256]{1,0:T(8,128)(2,1)} %constant.46.g_ref, bf16[256,256]{1,0:T(8,128)(2,1)} %constant.47.f2_ref, f32[2,128,128]{2,1,0:T(8,128)} %constant.34.clone.tw_ref, ...), custom_call_target="tpu_custom_call" | custom-call | tf_op jit(solution)/shard_map/backward_scatter/pallas_call | solution.py:565
  139.8 0.0 copy-start.1
  139.8 1.8 %reshape.63 = f32[1,2,64,2048]{3,1,2,0:T(2,128)S(1)} reshape(f32[2,64,16,128]{3,2,0,1:T(8,128)} %bitcast.29) | data formatting | bytes 2097152 | tf_op jit(solution)/shard_map/reshape | solution.py:580
  141.6 1.6 %copy.21 = f32[1,2,64,2048]{3,2,1,0:T(8,128)} copy(f32[1,2,64,2048]{3,1,2,0:T(2,128)S(1)} %reshape.63) | data formatting | bytes 2097152
  143.2 0.0 copy-done.1
  143.2 0.6 copy.28
Async XLA Ops:
  0.6 7.0 %copy-start = (bf16[1,1,64,8192]{3,2,1,0:T(8,128)(2,1)S(1)}, bf16[1,1,64,8192]{3,2,1,0:T(8,128)(2,1)}, u32[]{:S(2)}) copy-start(bf16[1,1,64,8192]{3,2,1,0:T(8,128)(2,1)} %param.17) | copy-start | bytes 3145732
  139.8 3.4 %copy-start.1 = (f32[16,2,512]{2,1,0:T(2,128)S(1)}, f32[16,2,512]{2,1,0:T(2,128)}, u32[]{:S(2)}) copy-start(f32[16,2,512]{2,1,0:T(2,128)} %get-tuple-element.4) | copy-start | bytes 196612

commit v3 on v2

--- a/solution.py
+++ b/solution.py
@@ -267,11 +267,14 @@
 
 def facet_factor(window, shift_cells, subgrids):
     length = window.shape[0]
-    positions = jnp.arange(length, dtype=jnp.int32)
-    turn_count = positions * shift_cells % length
+    rows = length // subgrids
+    grid = window.reshape(subgrids, rows)
+    grid = jnp.concatenate([grid, grid], axis=1)
+    high = lax.broadcasted_iota(jnp.int32, grid.shape, 0)
+    low = lax.broadcasted_iota(jnp.int32, grid.shape, 1) % rows
+    turn_count = (high * rows + low) * shift_cells % length
     angles = 2.0 * math.pi / length * turn_count.astype(jnp.float32)
-    both = jnp.stack([window * jnp.cos(angles), -window * jnp.sin(angles)]).reshape(2, subgrids, -1)
-    return jnp.concatenate([both, both], axis=2)
+    return jnp.stack([grid * jnp.cos(angles), -grid * jnp.sin(angles)])
 
 
 def spread(cells, length, taps):
@@ -306,7 +309,7 @@
 
 def middle_kernel(
     contrib_ref, u_ref, v_ref, plane_ref, obs_ref, taps_ref, table_ref, res_ref, out_ref,
-    r0, acc0, r1, acc1, r2, fin, adj, phase, s0, d0, s1, d1, s2, d2, sg, dg,
+    r0, acc0, r1, acc1, r2, fin, adj, phase, row_table, column_table, s0, d0, s1, d1, s2, d2, sg, dg,
 ):
     pairs = contrib_ref.shape[1]
     per, vis = u_ref.shape
@@ -374,6 +377,26 @@
         sine = jnp.where(hit, table_ref[1, k], sine)
     phase[0] = cosine
     phase[1] = sine
+
+    def weights(cells, position, length):
+        count = taps_ref.shape[0]
+        offset = position - cells + count // 2
+        offset = jnp.where(offset < 0, offset + length, jnp.where(offset >= length, offset - length, offset))
+        out = jnp.zeros(offset.shape, jnp.float32)
+        for t in range(count):
+            out = jnp.where(offset == t, taps_ref[t], out)
+        return out
+
+    def prepare(s, carry):
+        at = pl.ds(s, 1)
+        row = lax.broadcasted_iota(jnp.int32, (rows, vis), 0)
+        half = lax.broadcasted_iota(jnp.int32, (pairs, vis), 0)
+        col = jnp.concatenate([2 * half, 2 * half + 1], axis=0)
+        row_table[s] = weights(u_ref[at, :], row, rows)
+        column_table[s] = weights(v_ref[at, :], col, cols).astype(jnp.bfloat16)
+        return carry
+
+    lax.fori_loop(0, per, prepare, 0)
 
     for k in range(2):
         for p in range(2):
@@ -388,23 +411,11 @@
             total = acc1[p, bits[1 - p], t].astype(jnp.float32) + r2[p, t].astype(jnp.float32)
             fin[p, pl.ds(t, per, stride=pairs), :] = total
 
-    def weights(cells, position, length):
-        count = taps_ref.shape[0]
-        offset = position - cells + count // 2
-        offset = jnp.where(offset < 0, offset + length, jnp.where(offset >= length, offset - length, offset))
-        out = jnp.zeros(offset.shape, jnp.float32)
-        for t in range(count):
-            out = jnp.where(offset == t, taps_ref[t], out)
-        return out
-
-    def one(s, carry):
+    def one(s):
         at = pl.ds(s, 1)
         where = pl.ds(pl.multiple_of(s * pairs, pairs), pairs)
-        row = lax.broadcasted_iota(jnp.int32, (rows, vis), 0)
-        half = lax.broadcasted_iota(jnp.int32, (pairs, vis), 0)
-        col = jnp.concatenate([2 * half, 2 * half + 1], axis=0)
-        row_weights = weights(u_ref[at, :], row, rows)
-        column_weights = weights(v_ref[at, :], col, cols).astype(jnp.bfloat16)
+        row_weights = row_table[s]
+        column_weights = column_table[s]
         real, imag = fin[0, where, :], fin[1, where, :]
         grid = jnp.concatenate(
             [
@@ -432,9 +443,13 @@
         )
         adj[0, where, :] = jnp.concatenate([back[:pairs, :rows], back[pairs:, :rows]], axis=1)
         adj[1, where, :] = jnp.concatenate([back[:pairs, rows:], back[pairs:, rows:]], axis=1)
+
+    def four(block, carry):
+        for k in range(4):
+            one(4 * block + k)
         return carry
 
-    lax.fori_loop(0, per, one, 0)
+    lax.fori_loop(0, per // 4, four, 0)
 
     def gather(step, p, device, peer):
         block = out_ref.at[p, :, rows_of(device)]
@@ -496,6 +511,8 @@
             pltpu.VMEM((2, per * pairs, lanes), jnp.float32),
             pltpu.VMEM((2, per * pairs, lanes), jnp.float32),
             pltpu.VMEM((2, per, vis), jnp.float32),
+            pltpu.VMEM((per, lanes // 2, vis), jnp.float32),
+            pltpu.VMEM((per, 2 * pairs, vis), jnp.bfloat16),
             dma(2, 4), dma(2, 4), dma(2, 2), dma(2, 2), dma(2), dma(2), dma(3, 2, 8), dma(2, 8),
         ],
         compiler_params=pltpu.CompilerParams(collective_id=2, has_side_effects=True),

time: 144 us -> 139 us (0.965)
  Pallas kernels: 131 us -> 126 us
    pallas_call x1, Pallas kernels: 41.6 us -> 36.7 us  [fused_middle(): pl.pallas_call(middle_kernel, out_shape=(jax.ShapeDtypeStruct((per, 2, vi...]
    mul x1, other arithmetic: 2.1 us -> 0.35 us  [facet_factor(): return jnp.stack([grid * jnp.cos(angles), -grid * jnp.sin(angles)])]
    unnamed x0 -> x1, other arithmetic: none -> 1.48 us
    unnamed x8 -> x9, local copies, waits for them, and re-layouts: 4.62 us -> 5.13 us
where the time goes in v3:
time: 139 us
  Pallas kernels  126 us (91%)
  local copies, waits for them, and re-layouts  8.52 us (6%)
  other arithmetic  3.08 us (2%)
  between operations  1.45 us (1%)
    pallas_call x1, Pallas kernels, local(): pl.pallas_call(functools.partial(backward_kernel, n), out_shape=jax.Shape...  45.4 us
    pallas_call x1, Pallas kernels, local(): pl.pallas_call(functools.partial(forward_kernel, n), out_shape=jax.ShapeD...  43.9 us
    pallas_call x1, Pallas kernels, fused_middle(): pl.pallas_call(middle_kernel, out_shape=(jax.ShapeDtypeStruct((per, 2, vi...  36.7 us
    unnamed x9, local copies, waits for them, and re-layouts  5.13 us

profile of v3, /device:TPU:0, one launch (start us, length us, event | category | flops | bytes accessed | tf_op | source)
XLA Modules:
  0.0 139.1 jit_solution(12101220225792294991)
XLA Ops:
  0.6 0.0 copy-start
  1.4 0.7 fusion.3
  2.1 0.6 pad_maximum_fusion.2.table_ref
  2.7 0.5 broadcast.269
  3.2 1.5 %reduce.3 = f32[8192]{0:T(1024)S(1)} reduce(f32[1,8192]{1,0:T(1,128)} %param.18, f32[]{:T(128)} %broadcast.269), dimensions={0}, to_apply=%param.18.reduce_sub_computation.3 | reduce | bytes 65540 | tf_op args[2]
  4.7 0.1 concatenate.19
  4.7 0.4 cosine_multiply_fusion
  5.1 0.7 pad_maximum_fusion.fac_ref
  5.8 1.1 copy.23
  6.9 0.8 copy_bitcast_fusion.x_ref
  7.7 0.0 copy-done
  7.7 1.3 copy.24
  9.0 43.9 %gather_forward.1.contrib_ref = bf16[2,32,128,128]{3,2,1,0:T(8,128)(2,1)} custom-call(bf16[64,2,16,128]{3,2,1,0:T(8,128)(2,1)} %copy_bitcast_fusion.x_ref, bf16[64,64,128]{2,1,0:T(8,128)(2,1)} %bitcast.27, bf16[128,128]{1,0:T(8,128)(2,1)} %constant.57.f1_ref, bf16[256,256]{1,0:T(8,128)(2,1)} %constant.58.g_ref, f32[2,64,128]{2,1,0:T(8,128)} %constant.46.clone.tw_ref, ...), custom_call_target="tpu_custom_call" | custom-call | tf_op jit(solution)/shard_map/gather_forward/pallas_call | solution.py:553
  53.0 36.7 %degrid_exchange.1 = (f32[16,2,512]{2,1,0:T(2,128)}, bf16[2,32,128,128]{3,2,1,0:T(8,128)(2,1)}) custom-call(bf16[2,32,128,128]{3,2,1,0:T(8,128)(2,1)} %gather_forward.1.contrib_ref, s32[16,512]{1,0:T(8,128)} %bitcast.35, s32[16,512]{1,0:T(8,128)} %bitcast.36, s32[16,512]{1,0:T(8,128)} %bitcast.37, f32[16,2,512]{2,1,0:T(2,128)} %bitcast.33, f32[7]{0:T(128)} %taps_ref.1, ...), custom_call_target="tpu_custom_call" | custom-call | tf_op jit(solution)/shard_map/degrid_exchange/pallas_call | solution.py:501
  89.7 45.4 %backward_scatter.1 = f32[64,2,16,128]{3,2,1,0:T(8,128)} custom-call(bf16[2,32,128,128]{3,2,1,0:T(8,128)(2,1)} %get-tuple-element.5.a_ref, bf16[64,64,128]{2,1,0:T(8,128)(2,1)} %bitcast.28, bf16[256,256]{1,0:T(8,128)(2,1)} %constant.59.g_ref, bf16[256,256]{1,0:T(8,128)(2,1)} %constant.60.f2_ref, f32[2,128,128]{2,1,0:T(8,128)} %constant.47.clone.tw_ref, ...), custom_call_target="tpu_custom_call" | custom-call | tf_op jit(solution)/shard_map/backward_scatter/pallas_call | solution.py:582
  135.1 0.0 copy-start.1
  135.1 1.8 %reshape.288 = f32[1,2,64,2048]{3,1,2,0:T(2,128)S(1)} reshape(f32[2,64,16,128]{3,2,0,1:T(8,128)} %bitcast.29) | data formatting | bytes 2097152 | tf_op jit(solution)/shard_map/reshape | solution.py:597
  136.9 1.6 %copy.21 = f32[1,2,64,2048]{3,2,1,0:T(8,128)} copy(f32[1,2,64,2048]{3,1,2,0:T(2,128)S(1)} %reshape.288) | data formatting | bytes 2097152
  138.5 0.0 copy-done.1
  138.5 0.6 copy.28
  (3 shorter events, 0.0 us)
Async XLA Ops:
  0.6 7.1 %copy-start = (bf16[1,1,64,8192]{3,2,1,0:T(8,128)(2,1)S(1)}, bf16[1,1,64,8192]{3,2,1,0:T(8,128)(2,1)}, u32[]{:S(2)}) copy-start(bf16[1,1,64,8192]{3,2,1,0:T(8,128)(2,1)} %param.17) | copy-start | bytes 3145732
  135.1 3.4 %copy-start.1 = (f32[16,2,512]{2,1,0:T(2,128)S(1)}, f32[16,2,512]{2,1,0:T(2,128)}, u32[]{:S(2)}) copy-start(f32[16,2,512]{2,1,0:T(2,128)} %get-tuple-element.4) | copy-start | bytes 196612
